TPU v7x, 256 devices: a whole 4x4x8 slice. The times are simulated.
256 devices in a mesh: row: 4 (over x_lo, core), col: 64 (over y, z, x_hi).
Axes of the slice: x: 4 (x_hi: 2, x_lo: 2; x = x_hi * 2 + x_lo), y: 4, z: 8, core: 2. Of those that a mesh axis runs over, the one named last changes fastest.
Arguments:
- old_table: float32 [64, 4096, 128], P('col', 'row'), may hold values from -1 to 1
- old_blocks: int32 [64, 32], P('col', 'row'), may hold values from 0 to 31, as said below
- new_blocks: int32 [64, 32], P('col', 'row'), may hold values from 0 to 31, as said below
- bag_row_index: int32 [4096, 64, 64], P(None, 'col'), may hold values from 0 to 4095
- bag_length: int32 [4096, 64], P(None, 'col'), may hold values from 1 to 64
- dense: bfloat16 [4096, 128], P(('row', 'col')), may hold values from -6 to 6
- w_first: bfloat16 [2208, 1024], replicated, may hold values from -0.25 to 0.25
- w_second: bfloat16 [1024, 1024], replicated, may hold values from -0.25 to 0.25
- w_out: bfloat16 [1024], replicated, may hold values from -0.75 to 0.75
Outputs:
- logits: float32 [4096], P(('row', 'col'))
- new_tables: float32 [64, 4096, 128], P('col', 'row')
Inputs may be any that keep to these rules, and one draw needn't show every extreme that they name: `old_blocks`: for each table a permutation of the blocks; row device r holds positions r * 8 to (r + 1) * 8 - 1. For each table a permutation of the blocks; for every ordered pair of row devices, exactly 2 of the blocks that the first holds in old_blocks lie on the second in new_blocks.
All inputs are finite; a program needn't handle non-finite values.
Results may differ from a plain program's by a relative error of at most 0.0069.
Values sent between devices are 32-bit elements; how exact they have to be, the bound alone decides.
No kernel may reach another device: no remote copies, remote signals or barrier semaphores. Data moves between devices by JAX's collectives and lax.ppermute only.
A program may use at most 64 MiB of HBM per device.

v0:
```python
import functools

import jax
import jax.numpy as jnp
from jax import lax
from jax.experimental import pallas as pl
from jax.experimental.pallas import tpu as pltpu
from jax.sharding import PartitionSpec as P


BLK = 128
BF16 = jnp.bfloat16
F32 = jnp.float32


def halves(x):
    top = x.astype(BF16)
    rest = (x - top.astype(F32)).astype(BF16)
    return top, rest


def in_vmem(x):
    return pltpu.with_memory_space_constraint(x, pltpu.VMEM)


def in_hbm(x):
    return pltpu.with_memory_space_constraint(x, pltpu.HBM)


def count_kernel(rank_ref, index_hbm, length_hbm, counts_ref, index, length, staged, sems):
    bag, share = index.shape
    blocks = counts_ref.shape[0]
    group = 128
    pitch = staged.shape[0] // group
    start = pl.multiple_of(rank_ref[0] * share, 128)
    fetch_index = pltpu.make_async_copy(index_hbm.at[:, pl.ds(start, share)], index, sems.at[0])
    fetch_length = pltpu.make_async_copy(length_hbm.at[:, pl.ds(start, share)], length, sems.at[1])
    fetch_index.start()
    fetch_length.start()
    fetch_index.wait()
    fetch_length.wait()
    place = lax.broadcasted_iota(jnp.int32, (bag, group), 0)
    offset_order = lax.broadcasted_iota(jnp.int32, (2 * bag, BLK), 1).astype(F32).astype(BF16)
    block_order = lax.broadcasted_iota(jnp.int32, (2 * blocks, 2 * bag), 0)
    one = jnp.ones((), BF16)
    none = jnp.zeros((), BF16)

    def some(step, carry):
        base = pl.multiple_of(step * group, group)
        rows = index[:, pl.ds(base, group)]
        rows = jnp.where(place < length[:, pl.ds(base, group)], rows, -1)
        offset = (rows & (BLK - 1)).astype(F32).astype(BF16)
        rows = jnp.transpose(rows, (1, 0))
        block = jnp.where(rows < 0, -1, lax.shift_right_arithmetic(rows, 7))
        second = jnp.where(block < 0, -1, block + blocks)
        for first in range(0, group, 16):
            key = jnp.concatenate([block[first : first + 8], second[first + 8 : first + 16]], axis=1)
            for k in range(8):
                n = first + k
                column = jnp.concatenate([offset[:, n : n + 1], offset[:, n + 8 : n + 9]], axis=0)
                in_block = jnp.where(key[k : k + 1] == block_order, 1.0, 0.0).astype(BF16)
                at_offset = jnp.where(column == offset_order, one, none)
                found = jnp.dot(in_block, at_offset, preferred_element_type=F32)
                staged[n * pitch : n * pitch + blocks, :] = found[:blocks]
                staged[(n + 8) * pitch : (n + 8) * pitch + blocks, :] = found[blocks:]
            for b in range(blocks):
                sixteen = staged[pl.ds(first * pitch + b, 16, stride=pitch), :].astype(BF16)
                counts_ref[b, pl.ds(pl.multiple_of(base + first, 16), 16), :] = sixteen
        return carry

    lax.fori_loop(0, share // group, some, 0)


def count_bags(rank, index, length, share, blocks):
    bag = index.shape[0]
    hbm = pl.BlockSpec(memory_space=pltpu.HBM)
    return pl.pallas_call(
        count_kernel,
        in_specs=[pl.BlockSpec(memory_space=pltpu.SMEM), hbm, hbm],
        out_specs=pl.BlockSpec(memory_space=pltpu.VMEM),
        out_shape=pltpu.VMEM((blocks, share, BLK), BF16),
        scratch_shapes=[
            pltpu.VMEM((bag, share), jnp.int32),
            pltpu.VMEM((1, share), jnp.int32),
            pltpu.VMEM((128 * (blocks + 4), BLK), F32),
            pltpu.SemaphoreType.DMA((2,)),
        ],
        cost_estimate=pl.CostEstimate(
            flops=40 << 30, bytes_accessed=8388608, transcendentals=0
        ),
        compiler_params=pltpu.CompilerParams(vmem_limit_bytes=16 << 20),
        name="count_bags",
    )(rank, in_hbm(index), in_hbm(length))


def pool_kernel(first_slot, has_prior, held_ref, counts_ref, *refs):
    refs = list(refs)
    split_rows = refs.pop()
    pooled_ref = refs.pop()
    prior_ref = refs.pop() if has_prior else None
    slots, _, width = refs[0].shape
    for k, part in enumerate(refs):
        for s in range(slots):
            at = (k * slots + s) * BLK
            top, rest = halves(part[s])
            split_rows[at : at + BLK, :width] = top
            split_rows[at : at + BLK, width:] = rest
    total = len(refs) * slots
    left = jnp.concatenate([counts_ref[held_ref[first_slot + q]] for q in range(total)], axis=1)
    found = jnp.dot(left, split_rows[...], preferred_element_type=F32)
    found = found[:, :width] + found[:, width:]
    pooled_ref[...] = found + prior_ref[...] if has_prior else found


def pool(held, first_slot, counts, parts, prior, keep):
    _, share, _ = counts.shape
    slots, _, width = parts[0].shape
    vmem = pl.BlockSpec(memory_space=pltpu.VMEM)
    arrays = [counts, *parts] + ([] if prior is None else [prior])
    return pl.pallas_call(
        functools.partial(pool_kernel, first_slot, prior is not None),
        in_specs=[pl.BlockSpec(memory_space=pltpu.SMEM)] + [vmem] * len(arrays),
        out_specs=vmem,
        out_shape=pltpu.VMEM((share, width), F32) if keep else pltpu.HBM((share, width), F32),
        scratch_shapes=[pltpu.VMEM((len(parts) * slots * BLK, 2 * width), BF16)],
        cost_estimate=pl.CostEstimate(
            flops=2 * share * len(parts) * slots * BLK * 2 * width,
            bytes_accessed=4 << 20,
            transcendentals=0,
        ),
        compiler_params=pltpu.CompilerParams(vmem_limit_bytes=24 << 20),
        name="pool",
    )(held, *[in_vmem(a) for a in arrays])


def move_kernel(held_ref, wanted_ref, part0, part1, part2, part3, moved_ref, target, sem):
    parts = (part0, part1, part2, part3)
    slots = part0.shape[0]
    for b in range(len(parts) * slots):
        target[b] = -1
    for s in range(slots):
        target[wanted_ref[s]] = s
    for k, part in enumerate(parts):
        for s in range(slots):
            goal = target[held_ref[k * slots + s]]

            @pl.when(goal >= 0)
            def _(part=part, s=s, goal=goal):
                pltpu.make_async_copy(part.at[s], moved_ref.at[goal], sem).start()

    pltpu.make_async_copy(part0, moved_ref, sem).wait()


def move_blocks(held, wanted, parts):
    slots, _, width = parts[0].shape
    smem = pl.BlockSpec(memory_space=pltpu.SMEM)
    hbm = pl.BlockSpec(memory_space=pltpu.HBM)
    return pl.pallas_call(
        move_kernel,
        in_specs=[smem, smem] + [pl.BlockSpec(memory_space=pltpu.VMEM)] * 4,
        out_specs=hbm,
        out_shape=jax.ShapeDtypeStruct((slots, BLK, width), F32),
        scratch_shapes=[pltpu.SMEM((len(parts) * slots,), jnp.int32), pltpu.SemaphoreType.DMA],
        compiler_params=pltpu.CompilerParams(vmem_limit_bytes=4 << 20),
        name="move_blocks",
    )(held, wanted, *[in_vmem(part) for part in parts])


def top_kernel(
    pooled_ref, dense_ref, first_hbm, second_hbm, out_ref, logits_ref,
    first_ref, second_ref, gram, joined, sems,
):
    samples, width = dense_ref.shape
    tables = pooled_ref.shape[0] // samples
    pitch = gram.shape[0] // samples
    inputs = first_ref.shape[0]
    fetch_first = pltpu.make_async_copy(first_hbm, first_ref, sems.at[0])
    fetch_second = pltpu.make_async_copy(second_hbm, second_ref, sems.at[1])
    fetch_first.start()
    fetch_second.start()
    whole = inputs // 128 * 128
    dense = dense_ref[...].astype(F32)
    for s in range(samples):
        top, rest = halves(pooled_ref[pl.ds(s, tables, stride=samples), :])
        own = jnp.broadcast_to(dense[s : s + 1], (8, width)).astype(BF16)
        none = jnp.zeros((8, width), BF16)
        tall_top = jnp.concatenate([top, own], axis=0)
        tall_rest = jnp.concatenate([rest, none], axis=0)
        left = jnp.concatenate([tall_top, tall_rest, tall_top], axis=1)
        right = jnp.concatenate([top, top, rest], axis=1)
        found = lax.dot_general(
            left, right, (((1,), (1,)), ((), ())), preferred_element_type=F32
        )
        gram[s * pitch : (s + 1) * pitch, :tables] = found * width ** (-0.5)
    lane = lax.broadcasted_iota(jnp.int32, (samples, 128), 1)
    joined[:, :width] = dense_ref[...]
    at = width
    filling = jnp.zeros((samples, 128), F32)
    for i in range(-1, tables - 1):
        row = tables if i < 0 else i
        start = 0 if i < 0 else i + 1
        line = gram[pl.ds(row, samples, stride=pitch), :]
        shift = (at - start) % 128
        line = pltpu.roll(line, shift, 1) if shift else line
        filling = jnp.where(lane >= at % 128, line, filling)
        after = at + tables - start
        if after // 128 != at // 128:
            base = at // 128 * 128
            joined[:, base : base + 128] = filling.astype(BF16)
            filling = line
        at = after
    base = at // 128 * 128
    if at % 128:
        joined[:, base : base + 128] = jnp.where(lane < at % 128, filling, 0.0).astype(BF16)
    fetch_first.wait()
    hidden = jnp.dot(joined[:, :whole], first_ref[:whole], preferred_element_type=F32)
    if inputs > whole:
        last = jnp.dot(joined[:, whole:inputs], first_ref[whole:], preferred_element_type=F32)
        hidden = hidden + last
    hidden = jnp.maximum(hidden, 0.0).astype(BF16)
    fetch_second.wait()
    hidden = jnp.dot(hidden, second_ref[...], preferred_element_type=F32)
    hidden = jnp.maximum(hidden, 0.0).astype(BF16)
    last = jnp.broadcast_to(out_ref[...], (16, hidden.shape[1]))
    answer = lax.dot_general(last, hidden, (((1,), (1,)), ((), ())), preferred_element_type=F32)
    logits_ref[...] = answer[:1]


def top_of_model(pooled, dense, w_first, w_second, w_out):
    samples, _ = dense.shape
    tables = pooled.shape[0] // samples
    inputs, _ = w_first.shape
    padded = -(-inputs // 128) * 128
    hbm = pl.BlockSpec(memory_space=pltpu.HBM)
    vmem = pl.BlockSpec(memory_space=pltpu.VMEM)
    return pl.pallas_call(
        top_kernel,
        in_specs=[vmem, vmem, hbm, hbm, vmem],
        out_specs=vmem,
        out_shape=jax.ShapeDtypeStruct((1, samples), F32),
        scratch_shapes=[
            pltpu.VMEM(w_first.shape, BF16),
            pltpu.VMEM(w_second.shape, BF16),
            pltpu.VMEM((samples * (tables + 8), 128), F32),
            pltpu.VMEM((samples, padded), BF16),
            pltpu.SemaphoreType.DMA((2,)),
        ],
        compiler_params=pltpu.CompilerParams(vmem_limit_bytes=16 << 20),
        name="top_of_model",
    )(in_vmem(pooled), dense, in_hbm(w_first), in_hbm(w_second), w_out.reshape(1, -1))


def shards(
    old_table, old_blocks, new_blocks, bag_row_index, bag_length, dense, w_first, w_second, w_out
):
    slots = old_blocks.shape[1]
    width = old_table.shape[2]
    rows = lax.axis_size("row")
    rank = lax.axis_index("row")
    own = old_table[0].reshape(slots, BLK, width)
    other_core = [(k, k ^ 1) for k in range(rows)]
    other_chip = [(k, k ^ 2) for k in range(rows)]
    both = [(k, k ^ 3) for k in range(rows)]
    ids = old_blocks[0]
    across = lax.ppermute(own, "row", other_chip)
    beside = lax.ppermute(own, "row", other_core)
    named = [ids]
    for pairs in (other_core, other_chip, both):
        named.append(lax.ppermute(ids, "row", pairs))
    held = jnp.concatenate(named)
    share = bag_row_index.shape[0] // rows
    counts = count_bags(
        rank.astype(jnp.int32)[None],
        jnp.transpose(bag_row_index[:, 0, :]),
        jnp.transpose(bag_length),
        share,
        rows * slots,
    )
    far = lax.ppermute(across, "row", other_core)
    pooled = pool(held, 0, counts, (own, beside, across), None, True)
    pooled = pool(held, 3 * slots, counts, (far,), pooled, False)
    moved = move_blocks(held, new_blocks[0], (own, beside, across, far))
    cols = lax.axis_size("col")
    pooled = pooled.reshape(cols, share // cols, width)
    spread = lax.all_to_all(pooled, "col", split_axis=0, concat_axis=0, tiled=True)
    logits = top_of_model(spread.reshape(share, width), dense, w_first, w_second, w_out)
    return logits.reshape(-1), moved.reshape(1, slots * BLK, width)


def solution(mesh):
    in_specs = (
        P("col", "row", None),
        P("col", "row"),
        P("col", "row"),
        P(None, "col", None),
        P(None, "col"),
        P(("row", "col"), None),
        P(),
        P(),
        P(),
    )
    out_specs = (P(("row", "col")), P("col", "row", None))

    return jax.shard_map(shards, mesh=mesh, in_specs=in_specs, out_specs=out_specs, check_vma=False)
```

profile of v0, /device:TPU:8, one launch (start us, length us, event | category | flops | bytes accessed | tf_op | source)
XLA Modules:
  0.0 67.8 jit_solution(6793816603611734860)
XLA Ops:
  0.6 1.6 %collective-permute-start.3 = (f32[8,128,128]{2,1,0:T(8,128)}, f32[8,128,128]{2,1,0:T(8,128)S(1)}, u32[]{:S(2)}, u32[]{:S(2)}) collective-permute-start(f32[8,128,128]{2,1,0:T(8,128)} %bitcast.13), channel_id=1, source_target_pairs={{0,128},{64,192},{128,0},{192,64},{1,129},{65,193},{129,1},{193,65... | collective-permute-start | bytes 1572872 | tf_op jit(solution)/shard_map/ppermute | solution.py:265
  2.2 0.0 collective-permute-start
  2.2 0.5 collective-permute-start.1
  2.7 1.3 %collective-permute-start.2 = (s32[8]{0:T(128)}, s32[8]{0:T(128)S(1)}, u32[]{:S(2)}, u32[]{:S(2)}) collective-permute-start(s32[8]{0:T(128)} %bitcast.23), channel_id=1, source_target_pairs={{0,192},{64,128},{128,64},{192,0},{1,193},{65,129},{129,65},{193,1... | collective-permute-start | bytes 104 | tf_op jit(solution)/shard_map/ppermute | solution.py:269
  4.1 0.3 collective-permute-start.5
  4.4 10.2 %collective-permute-done.3.refs_2_.part2 = f32[8,128,128]{2,1,0:T(8,128)S(1)} collective-permute-done((f32[8,128,128]{2,1,0:T(8,128)}, f32[8,128,128]{2,1,0:T(8,128)S(1)}, u32[]{:S(2)}, u32[]{:S(2)}) %collective-permute-start.3) | collective-permute-done | bytes 524320 | tf_op jit(solution)/shard_map/ppermute | solution.py:265
  14.6 0.0 collective-permute-start.4
  14.6 0.0 copy-start.4
  14.6 0.0 copy-start
  14.6 10.1 %count_bags.1.counts_ref = bf16[32,1024,128]{2,1,0:T(8,128)(2,1)S(1)} custom-call(s32[1]{0:T(128)} %bitcast.1.rank_ref, s32[64,4096]{1,0:T(8,128)} %bitcast.25, s32[1,4096]{1,0:T(1,128)} %bitcast.26), custom_call_target="tpu_custom_call" | custom-call | flops 42949672960 | bytes 8388608 | tf_op jit(solution)/shard_map/count_bags/pallas_call | solution.py:77
  24.7 0.0 collective-permute-done
  24.8 0.0 collective-permute-done.1
  24.8 0.0 collective-permute-done.2
  24.8 0.0 copy-done.4
  24.8 0.1 pad_add_fusion.held_ref
  24.9 0.0 collective-permute-done.5.refs_1_.part1
  24.9 0.0 copy-done
  24.9 2.6 %pool.2.refs_1_ = f32[1024,128]{1,0:T(8,128)S(1)} custom-call(s32[32]{0:T(128)S(1)} %pad_add_fusion.held_ref, bf16[32,1024,128]{2,1,0:T(8,128)(2,1)S(1)} %count_bags.1.counts_ref, f32[8,128,128]{2,1,0:T(8,128)S(1)} %bitcast.15, f32[8,128,128]{2,1,0:T(8,128)S(1)} %collective-permute-done.5.refs_1_.part1, f32[8,128,128]{2,1,0:T(8,128)S(1)} %collective-permute-done.3.refs_2_.part2), custom_call_target="tpu_custom_call" | custom-call | flops 1610612736 | bytes 4194304 | tf_op jit(solution)/shard_map/pool/pallas_call | solution.py:120
  27.5 0.0 copy-start.3
  27.5 0.0 copy-start.2
  27.5 0.0 copy-start.1
  27.5 0.0 collective-permute-done.4.refs_0_.part3
  27.5 2.1 %pool.3 = f32[1024,128]{1,0:T(8,128)} custom-call(s32[32]{0:T(128)S(1)} %pad_add_fusion.held_ref, bf16[32,1024,128]{2,1,0:T(8,128)(2,1)S(1)} %count_bags.1.counts_ref, f32[8,128,128]{2,1,0:T(8,128)S(1)} %collective-permute-done.4.refs_0_.part3, f32[1024,128]{1,0:T(8,128)S(1)} %pool.2.refs_1_), custom_call_target="tpu_custom_call" | custom-call | flops 536870912 | bytes 4194304 | tf_op jit(solution)/shard_map/pool/pallas_call | solution.py:120
  29.6 14.6 %all-to-all-start = ((f32[64,16,128]{2,1,0:T(8,128)}), f32[64,16,128]{2,1,0:T(8,128)S(1)}, u32[]{:S(2)}, u32[]{:S(2)}) async-start(f32[64,16,128]{2,1,0:T(8,128)} %bitcast.18), calls=%async_computation | async-start | bytes 1048576 | tf_op jit(solution)/shard_map/all_to_all | solution.py:285
  44.2 0.0 copy-done.3
  44.2 0.0 copy-done.2
  44.3 1.4 %move_blocks.1 = f32[8,128,128]{2,1,0:T(8,128)} custom-call(s32[32]{0:T(128)S(1)} %pad_add_fusion.held_ref, s32[8]{0:T(128)S(1)} %bitcast.17, f32[8,128,128]{2,1,0:T(8,128)S(1)} %bitcast.16, f32[8,128,128]{2,1,0:T(8,128)S(1)} %collective-permute-done.5.refs_1_.part1, f32[8,128,128]{2,1,0:T(8,128)S(1)} %collective-permute-done.3.refs_2_.part2, ...), custom_call_target="tpu_custom_call" | custom-call | tf_op jit(solution)/shard_map/move_blocks/pallas_call | solution.py:158
  45.6 17.6 %all-to-all-done = f32[64,16,128]{2,1,0:T(8,128)S(1)} async-done(((f32[64,16,128]{2,1,0:T(8,128)}), f32[64,16,128]{2,1,0:T(8,128)S(1)}, u32[]{:S(2)}, u32[]{:S(2)}) %all-to-all-start) | async-done | bytes 524320 | tf_op jit(solution)/shard_map/all_to_all | solution.py:285
  63.2 0.0 copy-done.1
  63.2 4.6 %top_of_model.1 = f32[1,16]{1,0:T(1,128)} custom-call(f32[1024,128]{1,0:T(8,128)S(1)} %bitcast.12, bf16[16,128]{1,0:T(8,128)(2,1)S(1)} %copy-done.1, bf16[2208,1024]{1,0:T(8,128)(2,1)} %first_hbm.1, bf16[1024,1024]{1,0:T(8,128)(2,1)} %second_hbm.1, bf16[1,1024]{1,0:T(2,128)(2,1)S(1)} %reshape.21.out_ref), custom_call_target="tpu_custom_call" | custom-call | tf_op jit(solution)/shard_map/top_of_model/pallas_call | solution.py:236
  (1 shorter events, 0.0 us)
Async XLA Ops:
  0.6 14.0 %collective-permute-start.3 = (f32[8,128,128]{2,1,0:T(8,128)}, f32[8,128,128]{2,1,0:T(8,128)S(1)}, u32[]{:S(2)}, u32[]{:S(2)}) collective-permute-start(f32[8,128,128]{2,1,0:T(8,128)} %bitcast.13), channel_id=1, source_target_pairs={{0,128},{64,192},{128,0},{192,64},{1,129},{65,193},{129,1},{193,65... | collective-permute-start | bytes 1572872 | tf_op jit(solution)/shard_map/ppermute | solution.py:265
  2.2 22.5 %collective-permute-start = (s32[8]{0:T(128)}, s32[8]{0:T(128)S(1)}, u32[]{:S(2)}, u32[]{:S(2)}) collective-permute-start(s32[8]{0:T(128)} %bitcast.21), channel_id=1, source_target_pairs={{0,64},{64,0},{128,192},{192,128},{1,65},{65,1},{129,193},{193,129... | collective-permute-start | bytes 104 | tf_op jit(solution)/shard_map/ppermute | solution.py:269
  2.2 22.5 %collective-permute-start.1 = (s32[8]{0:T(128)}, s32[8]{0:T(128)S(1)}, u32[]{:S(2)}, u32[]{:S(2)}) collective-permute-start(s32[8]{0:T(128)} %bitcast.22), channel_id=1, source_target_pairs={{0,128},{64,192},{128,0},{192,64},{1,129},{65,193},{129,1},{193,65... | collective-permute-start | bytes 104 | tf_op jit(solution)/shard_map/ppermute | solution.py:269
  2.7 22.0 %collective-permute-start.2 = (s32[8]{0:T(128)}, s32[8]{0:T(128)S(1)}, u32[]{:S(2)}, u32[]{:S(2)}) collective-permute-start(s32[8]{0:T(128)} %bitcast.23), channel_id=1, source_target_pairs={{0,192},{64,128},{128,64},{192,0},{1,193},{65,129},{129,65},{193,1... | collective-permute-start | bytes 104 | tf_op jit(solution)/shard_map/ppermute | solution.py:269
  4.1 20.8 %collective-permute-start.5 = (f32[8,128,128]{2,1,0:T(8,128)}, f32[8,128,128]{2,1,0:T(8,128)S(1)}, u32[]{:S(2)}, u32[]{:S(2)}) collective-permute-start(f32[8,128,128]{2,1,0:T(8,128)} %bitcast.14), channel_id=1, source_target_pairs={{0,64},{64,0},{128,192},{192,128},{1,65},{65,1},{129,193},{193,129... | collective-permute-start | bytes 1572872 | tf_op jit(solution)/shard_map/ppermute | solution.py:266
  14.6 12.9 %collective-permute-start.4 = (f32[8,128,128]{2,1,0:T(8,128)S(1)}, f32[8,128,128]{2,1,0:T(8,128)S(1)}, u32[]{:S(2)}, u32[]{:S(2)}) collective-permute-start(f32[8,128,128]{2,1,0:T(8,128)S(1)} %collective-permute-done.3.refs_2_.part2), channel_id=1, source_target_pairs={{0,64},{64,0},{128,192},{192,128},{1,65},{65,1},{129,193},{193,129... | collective-permute-start | bytes 1572872 | tf_op jit(solution)/shard_map/ppermute | solution.py:279
  14.6 10.2 %copy-start.4 = (s32[1,8]{1,0:T(1,128)S(1)}, s32[1,8]{1,0:T(1,128)}, u32[]{:S(2)}) copy-start(s32[1,8]{1,0:T(1,128)} %param.10) | copy-start | bytes 100
  14.6 10.3 %copy-start = (f32[1,1024,128]{2,1,0:T(8,128)S(1)}, f32[1,1024,128]{2,1,0:T(8,128)}, u32[]{:S(2)}) copy-start(f32[1,1024,128]{2,1,0:T(8,128)} %param.9) | copy-start | bytes 1572868
  27.5 16.8 %copy-start.3 = (bf16[1024]{0:T(1024)(128)(2,1)S(1)}, bf16[1024]{0:T(1024)(128)(2,1)}, u32[]{:S(2)}) copy-start(bf16[1024]{0:T(1024)(128)(2,1)} %param.17) | copy-start | bytes 6148
  27.5 16.8 %copy-start.2 = (s32[1,8]{1,0:T(1,128)S(1)}, s32[1,8]{1,0:T(1,128)}, u32[]{:S(2)}) copy-start(s32[1,8]{1,0:T(1,128)} %param.11) | copy-start | bytes 100
  27.5 35.7 %copy-start.1 = (bf16[16,128]{1,0:T(8,128)(2,1)S(1)}, bf16[16,128]{1,0:T(8,128)(2,1)}, u32[]{:S(2)}) copy-start(bf16[16,128]{1,0:T(8,128)(2,1)} %dense_ref.1) | copy-start | bytes 12292
  29.6 33.6 %all-to-all-start = ((f32[64,16,128]{2,1,0:T(8,128)}), f32[64,16,128]{2,1,0:T(8,128)S(1)}, u32[]{:S(2)}, u32[]{:S(2)}) async-start(f32[64,16,128]{2,1,0:T(8,128)} %bitcast.18), calls=%async_computation | async-start | bytes 1048576 | tf_op jit(solution)/shard_map/all_to_all | solution.py:285
where the time goes:
time: 68.1 us; the launch traced here: 67.8 us
  waiting for transfers between devices  27.9 us (41%)
  Pallas kernels  20.8 us (31%)
  starting transfers between devices  18.3 us (27%)
  between operations  0.76 us (1%)
    all_to_all x1, waiting for transfers between devices, shards(): lax.all_to_all(pooled, 'col', split_axis=0, concat_axis=0, tiled=True)  17.6 us
    all_to_all x1, starting transfers between devices, shards(): lax.all_to_all(pooled, 'col', split_axis=0, concat_axis=0, tiled=True)  14.6 us
    ppermute x1, waiting for transfers between devices, shards(): across = lax.ppermute(own, 'row', other_chip)  10.2 us
    pallas_call x1, Pallas kernels, count_bags(): pl.pallas_call(count_kernel, in_specs=[pl.BlockSpec(memory_space=pltpu.SM...  10.1 us
    pallas_call x2, Pallas kernels, pool(): pl.pallas_call(functools.partial(pool_kernel, first_slot, prior is not No...  4.72 us
    pallas_call x1, Pallas kernels, top_of_model(): pl.pallas_call(top_kernel, in_specs=[vmem, vmem, hbm, hbm, vmem], out_spe...  4.6 us
    ppermute x3, starting transfers between devices, shards(): named.append(lax.ppermute(ids, 'row', pairs))  1.86 us
    ppermute x1, starting transfers between devices, shards(): across = lax.ppermute(own, 'row', other_chip)  1.58 us
  transfers between devices with their start and end apart: 7, of which 2 were waited for; matrix products, arithmetic and copies ran while one was open for 0% of the time, Pallas kernels for 21%

commit v1 on v0

--- a/solution.py
+++ b/solution.py
@@ -9,6 +9,7 @@
 
 
 BLK = 128
+FETCH = 256
 BF16 = jnp.bfloat16
 F32 = jnp.float32
 
@@ -30,7 +31,7 @@
 def count_kernel(rank_ref, index_hbm, length_hbm, counts_ref, index, length, staged, sems):
     bag, share = index.shape
     blocks = counts_ref.shape[0]
-    group = 128
+    group = 256
     pitch = staged.shape[0] // group
     start = pl.multiple_of(rank_ref[0] * share, 128)
     fetch_index = pltpu.make_async_copy(index_hbm.at[:, pl.ds(start, share)], index, sems.at[0])
@@ -82,7 +83,7 @@
         scratch_shapes=[
             pltpu.VMEM((bag, share), jnp.int32),
             pltpu.VMEM((1, share), jnp.int32),
-            pltpu.VMEM((128 * (blocks + 4), BLK), F32),
+            pltpu.VMEM((256 * (blocks + 4), BLK), F32),
             pltpu.SemaphoreType.DMA((2,)),
         ],
         cost_estimate=pl.CostEstimate(
@@ -174,11 +175,16 @@
     tables = pooled_ref.shape[0] // samples
     pitch = gram.shape[0] // samples
     inputs = first_ref.shape[0]
-    fetch_first = pltpu.make_async_copy(first_hbm, first_ref, sems.at[0])
-    fetch_second = pltpu.make_async_copy(second_hbm, second_ref, sems.at[1])
-    fetch_first.start()
-    fetch_second.start()
-    whole = inputs // 128 * 128
+    depth = second_ref.shape[0]
+    pieces = [(first_hbm, first_ref, at, min(FETCH, inputs - at)) for at in range(0, inputs, FETCH)]
+    layer = len(pieces)
+    pieces += [(second_hbm, second_ref, at, min(FETCH, depth - at)) for at in range(0, depth, FETCH)]
+    fetches = [
+        pltpu.make_async_copy(there.at[pl.ds(at, size)], here.at[pl.ds(at, size)], sems.at[k])
+        for k, (there, here, at, size) in enumerate(pieces)
+    ]
+    for fetch in fetches:
+        fetch.start()
     dense = dense_ref[...].astype(F32)
     for s in range(samples):
         top, rest = halves(pooled_ref[pl.ds(s, tables, stride=samples), :])
@@ -212,14 +218,20 @@
     base = at // 128 * 128
     if at % 128:
         joined[:, base : base + 128] = jnp.where(lane < at % 128, filling, 0.0).astype(BF16)
-    fetch_first.wait()
-    hidden = jnp.dot(joined[:, :whole], first_ref[:whole], preferred_element_type=F32)
-    if inputs > whole:
-        last = jnp.dot(joined[:, whole:inputs], first_ref[whole:], preferred_element_type=F32)
-        hidden = hidden + last
-    hidden = jnp.maximum(hidden, 0.0).astype(BF16)
-    fetch_second.wait()
-    hidden = jnp.dot(hidden, second_ref[...], preferred_element_type=F32)
+    hidden = jnp.zeros((samples, first_ref.shape[1]), F32)
+    for fetch, (_, _, at, size) in zip(fetches[:layer], pieces[:layer]):
+        fetch.wait()
+        whole = size // 128 * 128
+        for begin, count in ((at, whole), (at + whole, size - whole)):
+            if count:
+                ends = slice(begin, begin + count)
+                hidden += jnp.dot(joined[:, ends], first_ref[ends], preferred_element_type=F32)
+    value = jnp.maximum(hidden, 0.0).astype(BF16)
+    hidden = jnp.zeros((samples, second_ref.shape[1]), F32)
+    for fetch, (_, _, at, size) in zip(fetches[layer:], pieces[layer:]):
+        fetch.wait()
+        ends = slice(at, at + size)
+        hidden += jnp.dot(value[:, ends], second_ref[ends], preferred_element_type=F32)
     hidden = jnp.maximum(hidden, 0.0).astype(BF16)
     last = jnp.broadcast_to(out_ref[...], (16, hidden.shape[1]))
     answer = lax.dot_general(last, hidden, (((1,), (1,)), ((), ())), preferred_element_type=F32)
@@ -243,7 +255,7 @@
             pltpu.VMEM(w_second.shape, BF16),
             pltpu.VMEM((samples * (tables + 8), 128), F32),
             pltpu.VMEM((samples, padded), BF16),
-            pltpu.SemaphoreType.DMA((2,)),
+            pltpu.SemaphoreType.DMA((-(-inputs // FETCH) - (-w_second.shape[0] // FETCH),)),
         ],
         compiler_params=pltpu.CompilerParams(vmem_limit_bytes=16 << 20),
         name="top_of_model",

time: 68.1 us -> 66.8 us (0.981)
  Pallas kernels: 20.8 us -> 19.5 us
    pallas_call x1, Pallas kernels: 10.1 us -> 9.03 us  [count_bags(): pl.pallas_call(count_kernel, in_specs=[pl.BlockSpec(memory_space=pltpu.SM...]
  transfers between devices with their start and end apart: 7 -> 7, of which waited for: 2 -> 2; matrix products, arithmetic and copies ran while one was open for 0% -> 0% of each run, Pallas kernels for 21% -> 20%
where the time goes in v1:
time: 66.8 us; the launch traced here: 66.5 us
  waiting for transfers between devices  27.9 us (42%)
  Pallas kernels  19.5 us (29%)
  starting transfers between devices  18.3 us (27%)
  between operations  0.76 us (1%)
    all_to_all x1, waiting for transfers between devices, shards(): lax.all_to_all(pooled, 'col', split_axis=0, concat_axis=0, tiled=True)  17.6 us
    all_to_all x1, starting transfers between devices, shards(): lax.all_to_all(pooled, 'col', split_axis=0, concat_axis=0, tiled=True)  14.6 us
    ppermute x1, waiting for transfers between devices, shards(): across = lax.ppermute(own, 'row', other_chip)  10.2 us
    pallas_call x1, Pallas kernels, count_bags(): pl.pallas_call(count_kernel, in_specs=[pl.BlockSpec(memory_space=pltpu.SM...  9.03 us
    pallas_call x2, Pallas kernels, pool(): pl.pallas_call(functools.partial(pool_kernel, first_slot, prior is not No...  4.72 us
    pallas_call x1, Pallas kernels, top_of_model(): pl.pallas_call(top_kernel, in_specs=[vmem, vmem, hbm, hbm, vmem], out_spe...  4.37 us
    ppermute x3, starting transfers between devices, shards(): named.append(lax.ppermute(ids, 'row', pairs))  1.86 us
    ppermute x1, starting transfers between devices, shards(): across = lax.ppermute(own, 'row', other_chip)  1.58 us
  transfers between devices with their start and end apart: 7, of which 2 were waited for; matrix products, arithmetic and copies ran while one was open for 0% of the time, Pallas kernels for 20%

profile of v1, /device:TPU:8, one launch (start us, length us, event | category | flops | bytes accessed | tf_op | source)
XLA Modules:
  0.0 66.5 jit_solution(16403080935227852249)
XLA Ops:
  0.6 1.6 %collective-permute-start.3 = (f32[8,128,128]{2,1,0:T(8,128)}, f32[8,128,128]{2,1,0:T(8,128)S(1)}, u32[]{:S(2)}, u32[]{:S(2)}) collective-permute-start(f32[8,128,128]{2,1,0:T(8,128)} %bitcast.13), channel_id=1, source_target_pairs={{0,128},{64,192},{128,0},{192,64},{1,129},{65,193},{129,1},{193,65... | collective-permute-start | bytes 1572872 | tf_op jit(solution)/shard_map/ppermute | solution.py:277
  2.2 0.0 collective-permute-start
  2.2 0.5 collective-permute-start.1
  2.7 1.3 %collective-permute-start.2 = (s32[8]{0:T(128)}, s32[8]{0:T(128)S(1)}, u32[]{:S(2)}, u32[]{:S(2)}) collective-permute-start(s32[8]{0:T(128)} %bitcast.23), channel_id=1, source_target_pairs={{0,192},{64,128},{128,64},{192,0},{1,193},{65,129},{129,65},{193,1... | collective-permute-start | bytes 104 | tf_op jit(solution)/shard_map/ppermute | solution.py:281
  4.1 0.3 collective-permute-start.5
  4.4 10.2 %collective-permute-done.3.refs_2_.part2 = f32[8,128,128]{2,1,0:T(8,128)S(1)} collective-permute-done((f32[8,128,128]{2,1,0:T(8,128)}, f32[8,128,128]{2,1,0:T(8,128)S(1)}, u32[]{:S(2)}, u32[]{:S(2)}) %collective-permute-start.3) | collective-permute-done | bytes 524320 | tf_op jit(solution)/shard_map/ppermute | solution.py:277
  14.6 0.0 collective-permute-start.4
  14.6 0.0 copy-start.4
  14.6 0.0 copy-start
  14.6 9.0 %count_bags.1.counts_ref = bf16[32,1024,128]{2,1,0:T(8,128)(2,1)S(1)} custom-call(s32[1]{0:T(128)} %bitcast.1.rank_ref, s32[64,4096]{1,0:T(8,128)} %bitcast.25, s32[1,4096]{1,0:T(1,128)} %bitcast.26), custom_call_target="tpu_custom_call" | custom-call | flops 42949672960 | bytes 8388608 | tf_op jit(solution)/shard_map/count_bags/pallas_call | solution.py:78
  23.6 0.0 collective-permute-done
  23.7 0.0 collective-permute-done.1
  23.7 0.0 collective-permute-done.2
  23.7 0.0 copy-done.4
  23.7 0.1 pad_add_fusion.held_ref
  23.8 0.0 collective-permute-done.5.refs_1_.part1
  23.8 0.0 copy-done
  23.8 2.6 %pool.2.refs_1_ = f32[1024,128]{1,0:T(8,128)S(1)} custom-call(s32[32]{0:T(128)S(1)} %pad_add_fusion.held_ref, bf16[32,1024,128]{2,1,0:T(8,128)(2,1)S(1)} %count_bags.1.counts_ref, f32[8,128,128]{2,1,0:T(8,128)S(1)} %bitcast.15, f32[8,128,128]{2,1,0:T(8,128)S(1)} %collective-permute-done.5.refs_1_.part1, f32[8,128,128]{2,1,0:T(8,128)S(1)} %collective-permute-done.3.refs_2_.part2), custom_call_target="tpu_custom_call" | custom-call | flops 1610612736 | bytes 4194304 | tf_op jit(solution)/shard_map/pool/pallas_call | solution.py:121
  26.4 0.0 copy-start.3
  26.4 0.0 copy-start.2
  26.4 0.0 copy-start.1
  26.4 0.0 collective-permute-done.4.refs_0_.part3
  26.4 2.1 %pool.3 = f32[1024,128]{1,0:T(8,128)} custom-call(s32[32]{0:T(128)S(1)} %pad_add_fusion.held_ref, bf16[32,1024,128]{2,1,0:T(8,128)(2,1)S(1)} %count_bags.1.counts_ref, f32[8,128,128]{2,1,0:T(8,128)S(1)} %collective-permute-done.4.refs_0_.part3, f32[1024,128]{1,0:T(8,128)S(1)} %pool.2.refs_1_), custom_call_target="tpu_custom_call" | custom-call | flops 536870912 | bytes 4194304 | tf_op jit(solution)/shard_map/pool/pallas_call | solution.py:121
  28.5 14.6 %all-to-all-start = ((f32[64,16,128]{2,1,0:T(8,128)}), f32[64,16,128]{2,1,0:T(8,128)S(1)}, u32[]{:S(2)}, u32[]{:S(2)}) async-start(f32[64,16,128]{2,1,0:T(8,128)} %bitcast.18), calls=%async_computation | async-start | bytes 1048576 | tf_op jit(solution)/shard_map/all_to_all | solution.py:297
  43.1 0.0 copy-done.3
  43.1 0.0 copy-done.2
  43.2 1.4 %move_blocks.1 = f32[8,128,128]{2,1,0:T(8,128)} custom-call(s32[32]{0:T(128)S(1)} %pad_add_fusion.held_ref, s32[8]{0:T(128)S(1)} %bitcast.17, f32[8,128,128]{2,1,0:T(8,128)S(1)} %bitcast.16, f32[8,128,128]{2,1,0:T(8,128)S(1)} %collective-permute-done.5.refs_1_.part1, f32[8,128,128]{2,1,0:T(8,128)S(1)} %collective-permute-done.3.refs_2_.part2, ...), custom_call_target="tpu_custom_call" | custom-call | tf_op jit(solution)/shard_map/move_blocks/pallas_call | solution.py:159
  44.5 17.6 %all-to-all-done = f32[64,16,128]{2,1,0:T(8,128)S(1)} async-done(((f32[64,16,128]{2,1,0:T(8,128)}), f32[64,16,128]{2,1,0:T(8,128)S(1)}, u32[]{:S(2)}, u32[]{:S(2)}) %all-to-all-start) | async-done | bytes 524320 | tf_op jit(solution)/shard_map/all_to_all | solution.py:297
  62.1 0.0 copy-done.1
  62.1 4.4 %top_of_model.1 = f32[1,16]{1,0:T(1,128)} custom-call(f32[1024,128]{1,0:T(8,128)S(1)} %bitcast.12, bf16[16,128]{1,0:T(8,128)(2,1)S(1)} %copy-done.1, bf16[2208,1024]{1,0:T(8,128)(2,1)} %first_hbm.1, bf16[1024,1024]{1,0:T(8,128)(2,1)} %second_hbm.1, bf16[1,1024]{1,0:T(2,128)(2,1)S(1)} %reshape.21.out_ref), custom_call_target="tpu_custom_call" | custom-call | tf_op jit(solution)/shard_map/top_of_model/pallas_call | solution.py:248
  (1 shorter events, 0.0 us)
Async XLA Ops:
  0.6 14.0 %collective-permute-start.3 = (f32[8,128,128]{2,1,0:T(8,128)}, f32[8,128,128]{2,1,0:T(8,128)S(1)}, u32[]{:S(2)}, u32[]{:S(2)}) collective-permute-start(f32[8,128,128]{2,1,0:T(8,128)} %bitcast.13), channel_id=1, source_target_pairs={{0,128},{64,192},{128,0},{192,64},{1,129},{65,193},{129,1},{193,65... | collective-permute-start | bytes 1572872 | tf_op jit(solution)/shard_map/ppermute | solution.py:277
  2.2 21.4 %collective-permute-start = (s32[8]{0:T(128)}, s32[8]{0:T(128)S(1)}, u32[]{:S(2)}, u32[]{:S(2)}) collective-permute-start(s32[8]{0:T(128)} %bitcast.21), channel_id=1, source_target_pairs={{0,64},{64,0},{128,192},{192,128},{1,65},{65,1},{129,193},{193,129... | collective-permute-start | bytes 104 | tf_op jit(solution)/shard_map/ppermute | solution.py:281
  2.2 21.4 %collective-permute-start.1 = (s32[8]{0:T(128)}, s32[8]{0:T(128)S(1)}, u32[]{:S(2)}, u32[]{:S(2)}) collective-permute-start(s32[8]{0:T(128)} %bitcast.22), channel_id=1, source_target_pairs={{0,128},{64,192},{128,0},{192,64},{1,129},{65,193},{129,1},{193,65... | collective-permute-start | bytes 104 | tf_op jit(solution)/shard_map/ppermute | solution.py:281
  2.7 20.9 %collective-permute-start.2 = (s32[8]{0:T(128)}, s32[8]{0:T(128)S(1)}, u32[]{:S(2)}, u32[]{:S(2)}) collective-permute-start(s32[8]{0:T(128)} %bitcast.23), channel_id=1, source_target_pairs={{0,192},{64,128},{128,64},{192,0},{1,193},{65,129},{129,65},{193,1... | collective-permute-start | bytes 104 | tf_op jit(solution)/shard_map/ppermute | solution.py:281
  4.1 19.7 %collective-permute-start.5 = (f32[8,128,128]{2,1,0:T(8,128)}, f32[8,128,128]{2,1,0:T(8,128)S(1)}, u32[]{:S(2)}, u32[]{:S(2)}) collective-permute-start(f32[8,128,128]{2,1,0:T(8,128)} %bitcast.14), channel_id=1, source_target_pairs={{0,64},{64,0},{128,192},{192,128},{1,65},{65,1},{129,193},{193,129... | collective-permute-start | bytes 1572872 | tf_op jit(solution)/shard_map/ppermute | solution.py:278
  14.6 11.8 %collective-permute-start.4 = (f32[8,128,128]{2,1,0:T(8,128)S(1)}, f32[8,128,128]{2,1,0:T(8,128)S(1)}, u32[]{:S(2)}, u32[]{:S(2)}) collective-permute-start(f32[8,128,128]{2,1,0:T(8,128)S(1)} %collective-permute-done.3.refs_2_.part2), channel_id=1, source_target_pairs={{0,64},{64,0},{128,192},{192,128},{1,65},{65,1},{129,193},{193,129... | collective-permute-start | bytes 1572872 | tf_op jit(solution)/shard_map/ppermute | solution.py:291
  14.6 9.1 %copy-start.4 = (s32[1,8]{1,0:T(1,128)S(1)}, s32[1,8]{1,0:T(1,128)}, u32[]{:S(2)}) copy-start(s32[1,8]{1,0:T(1,128)} %param.10) | copy-start | bytes 100
  14.6 9.2 %copy-start = (f32[1,1024,128]{2,1,0:T(8,128)S(1)}, f32[1,1024,128]{2,1,0:T(8,128)}, u32[]{:S(2)}) copy-start(f32[1,1024,128]{2,1,0:T(8,128)} %param.9) | copy-start | bytes 1572868
  26.4 16.8 %copy-start.3 = (bf16[1024]{0:T(1024)(128)(2,1)S(1)}, bf16[1024]{0:T(1024)(128)(2,1)}, u32[]{:S(2)}) copy-start(bf16[1024]{0:T(1024)(128)(2,1)} %param.17) | copy-start | bytes 6148
  26.4 16.8 %copy-start.2 = (s32[1,8]{1,0:T(1,128)S(1)}, s32[1,8]{1,0:T(1,128)}, u32[]{:S(2)}) copy-start(s32[1,8]{1,0:T(1,128)} %param.11) | copy-start | bytes 100
  26.4 35.8 %copy-start.1 = (bf16[16,128]{1,0:T(8,128)(2,1)S(1)}, bf16[16,128]{1,0:T(8,128)(2,1)}, u32[]{:S(2)}) copy-start(bf16[16,128]{1,0:T(8,128)(2,1)} %dense_ref.1) | copy-start | bytes 12292
  28.5 33.6 %all-to-all-start = ((f32[64,16,128]{2,1,0:T(8,128)}), f32[64,16,128]{2,1,0:T(8,128)S(1)}, u32[]{:S(2)}, u32[]{:S(2)}) async-start(f32[64,16,128]{2,1,0:T(8,128)} %bitcast.18), calls=%async_computation | async-start | bytes 1048576 | tf_op jit(solution)/shard_map/all_to_all | solution.py:297

commit v2 on v1

--- a/solution.py
+++ b/solution.py
@@ -28,7 +28,23 @@
     return pltpu.with_memory_space_constraint(x, pltpu.HBM)
 
 
-def count_kernel(rank_ref, index_hbm, length_hbm, counts_ref, index, length, staged, sems):
+def pooled_part(ids, counts_ref, parts, split_rows):
+    slots, _, width = parts[0].shape
+    for k, part in enumerate(parts):
+        for s in range(slots):
+            at = (k * slots + s) * BLK
+            top, rest = halves(part[s])
+            split_rows[at : at + BLK, :width] = top
+            split_rows[at : at + BLK, width:] = rest
+    left = jnp.concatenate([counts_ref[b] for b in ids], axis=1)
+    found = jnp.dot(left, split_rows[...], preferred_element_type=F32)
+    return found[:, :width] + found[:, width:]
+
+
+def count_kernel(
+    rank_ref, ids_hbm, index_hbm, length_hbm, own_hbm, counts_ref, pooled_ref,
+    ids, index, length, staged, own, split_rows, sems,
+):
     bag, share = index.shape
     blocks = counts_ref.shape[0]
     group = 256
@@ -36,8 +52,12 @@
     start = pl.multiple_of(rank_ref[0] * share, 128)
     fetch_index = pltpu.make_async_copy(index_hbm.at[:, pl.ds(start, share)], index, sems.at[0])
     fetch_length = pltpu.make_async_copy(length_hbm.at[:, pl.ds(start, share)], length, sems.at[1])
+    fetch_ids = pltpu.make_async_copy(ids_hbm, ids, sems.at[3])
+    fetch_own = pltpu.make_async_copy(own_hbm, own, sems.at[2])
     fetch_index.start()
     fetch_length.start()
+    fetch_own.start()
+    fetch_ids.start()
     fetch_index.wait()
     fetch_length.wait()
     place = lax.broadcasted_iota(jnp.int32, (bag, group), 0)
@@ -70,28 +90,38 @@
         return carry
 
     lax.fori_loop(0, share // group, some, 0)
-
-
-def count_bags(rank, index, length, share, blocks):
+    fetch_own.wait()
+    fetch_ids.wait()
+    held = [ids[0, s] for s in range(own.shape[0])]
+    pooled_ref[...] = pooled_part(held, counts_ref, [own], split_rows)
+
+
+def count_bags(rank, ids, index, length, own, share, blocks):
     bag = index.shape[0]
     hbm = pl.BlockSpec(memory_space=pltpu.HBM)
     return pl.pallas_call(
         count_kernel,
-        in_specs=[pl.BlockSpec(memory_space=pltpu.SMEM), hbm, hbm],
-        out_specs=pl.BlockSpec(memory_space=pltpu.VMEM),
-        out_shape=pltpu.VMEM((blocks, share, BLK), BF16),
+        in_specs=[pl.BlockSpec(memory_space=pltpu.SMEM)] + [hbm] * 4,
+        out_specs=[pl.BlockSpec(memory_space=pltpu.VMEM)] * 2,
+        out_shape=[
+            pltpu.VMEM((blocks, share, BLK), BF16),
+            pltpu.VMEM((share, own.shape[2]), F32),
+        ],
         scratch_shapes=[
+            pltpu.SMEM(ids.shape, jnp.int32),
             pltpu.VMEM((bag, share), jnp.int32),
             pltpu.VMEM((1, share), jnp.int32),
             pltpu.VMEM((256 * (blocks + 4), BLK), F32),
-            pltpu.SemaphoreType.DMA((2,)),
+            pltpu.VMEM(own.shape, F32),
+            pltpu.VMEM((own.shape[0] * BLK, 2 * own.shape[2]), BF16),
+            pltpu.SemaphoreType.DMA((4,)),
         ],
         cost_estimate=pl.CostEstimate(
             flops=40 << 30, bytes_accessed=8388608, transcendentals=0
         ),
-        compiler_params=pltpu.CompilerParams(vmem_limit_bytes=16 << 20),
+        compiler_params=pltpu.CompilerParams(vmem_limit_bytes=20 << 20),
         name="count_bags",
-    )(rank, in_hbm(index), in_hbm(length))
+    )(rank, in_hbm(ids), in_hbm(index), in_hbm(length), in_hbm(own))
 
 
 def pool_kernel(first_slot, has_prior, held_ref, counts_ref, *refs):
@@ -99,17 +129,8 @@
     split_rows = refs.pop()
     pooled_ref = refs.pop()
     prior_ref = refs.pop() if has_prior else None
-    slots, _, width = refs[0].shape
-    for k, part in enumerate(refs):
-        for s in range(slots):
-            at = (k * slots + s) * BLK
-            top, rest = halves(part[s])
-            split_rows[at : at + BLK, :width] = top
-            split_rows[at : at + BLK, width:] = rest
-    total = len(refs) * slots
-    left = jnp.concatenate([counts_ref[held_ref[first_slot + q]] for q in range(total)], axis=1)
-    found = jnp.dot(left, split_rows[...], preferred_element_type=F32)
-    found = found[:, :width] + found[:, width:]
+    ids = [held_ref[first_slot + q] for q in range(len(refs) * refs[0].shape[0])]
+    found = pooled_part(ids, counts_ref, refs, split_rows)
     pooled_ref[...] = found + prior_ref[...] if has_prior else found
 
 
@@ -281,15 +302,17 @@
         named.append(lax.ppermute(ids, "row", pairs))
     held = jnp.concatenate(named)
     share = bag_row_index.shape[0] // rows
-    counts = count_bags(
+    counts, pooled = count_bags(
         rank.astype(jnp.int32)[None],
+        old_blocks,
         jnp.transpose(bag_row_index[:, 0, :]),
         jnp.transpose(bag_length),
+        own,
         share,
         rows * slots,
     )
     far = lax.ppermute(across, "row", other_core)
-    pooled = pool(held, 0, counts, (own, beside, across), None, True)
+    pooled = pool(held, slots, counts, (beside, across), pooled, True)
     pooled = pool(held, 3 * slots, counts, (far,), pooled, False)
     moved = move_blocks(held, new_blocks[0], (own, beside, across, far))
     cols = lax.axis_size("col")

time: 66.8 us -> 66.9 us (level)
    pallas_call x1, Pallas kernels: 9.03 us -> 9.8 us  [count_bags(): pl.pallas_call(count_kernel, in_specs=[pl.BlockSpec(memory_space=pltpu.SM...]
where the time goes in v2:
time: 66.9 us; the launch traced here: 66.6 us
  waiting for transfers between devices  27.9 us (42%)
  Pallas kernels  19.6 us (29%)
  starting transfers between devices  18.3 us (27%)
  between operations  0.77 us (1%)
    all_to_all x1, waiting for transfers between devices, shards(): lax.all_to_all(pooled, 'col', split_axis=0, concat_axis=0, tiled=True)  17.6 us
    all_to_all x1, starting transfers between devices, shards(): lax.all_to_all(pooled, 'col', split_axis=0, concat_axis=0, tiled=True)  14.6 us
    ppermute x1, waiting for transfers between devices, shards(): across = lax.ppermute(own, 'row', other_chip)  10.2 us
    pallas_call x1, Pallas kernels, count_bags(): pl.pallas_call(count_kernel, in_specs=[pl.BlockSpec(memory_space=pltpu.SM...  9.8 us
    pallas_call x1, Pallas kernels, top_of_model(): pl.pallas_call(top_kernel, in_specs=[vmem, vmem, hbm, hbm, vmem], out_spe...  4.36 us
    pallas_call x2, Pallas kernels, pool(): pl.pallas_call(functools.partial(pool_kernel, first_slot, prior is not No...  4.08 us
    ppermute x3, starting transfers between devices, shards(): named.append(lax.ppermute(ids, 'row', pairs))  1.86 us
    ppermute x1, starting transfers between devices, shards(): across = lax.ppermute(own, 'row', other_chip)  1.58 us
  transfers between devices with their start and end apart: 7, of which 2 were waited for; matrix products, arithmetic and copies ran while one was open for 0% of the time, Pallas kernels for 20%

profile of v2, /device:TPU:8, one launch (start us, length us, event | category | flops | bytes accessed | tf_op | source)
XLA Modules:
  0.0 66.6 jit_solution(1908536493643486207)
XLA Ops:
  0.6 1.6 %collective-permute-start.3 = (f32[8,128,128]{2,1,0:T(8,128)}, f32[8,128,128]{2,1,0:T(8,128)S(1)}, u32[]{:S(2)}, u32[]{:S(2)}) collective-permute-start(f32[8,128,128]{2,1,0:T(8,128)} %bitcast.13), channel_id=1, source_target_pairs={{0,128},{64,192},{128,0},{192,64},{1,129},{65,193},{129,1},{193,65... | collective-permute-start | bytes 1572872 | tf_op jit(solution)/shard_map/ppermute | solution.py:298
  2.2 0.0 collective-permute-start
  2.2 0.5 collective-permute-start.1
  2.7 1.3 %collective-permute-start.2 = (s32[8]{0:T(128)}, s32[8]{0:T(128)S(1)}, u32[]{:S(2)}, u32[]{:S(2)}) collective-permute-start(s32[8]{0:T(128)} %bitcast.23), channel_id=1, source_target_pairs={{0,192},{64,128},{128,64},{192,0},{1,193},{65,129},{129,65},{193,1... | collective-permute-start | bytes 104 | tf_op jit(solution)/shard_map/ppermute | solution.py:302
  4.1 0.3 collective-permute-start.5
  4.4 10.2 %collective-permute-done.3.refs_1_.part2 = f32[8,128,128]{2,1,0:T(8,128)S(1)} collective-permute-done((f32[8,128,128]{2,1,0:T(8,128)}, f32[8,128,128]{2,1,0:T(8,128)S(1)}, u32[]{:S(2)}, u32[]{:S(2)}) %collective-permute-start.3) | collective-permute-done | bytes 524320 | tf_op jit(solution)/shard_map/ppermute | solution.py:298
  14.6 0.0 collective-permute-start.4
  14.6 0.0 copy-start.4
  14.6 9.8 %count_bags.1 = (bf16[32,1024,128]{2,1,0:T(8,128)(2,1)S(1)}, f32[1024,128]{1,0:T(8,128)S(1)}) custom-call(s32[1]{0:T(128)} %bitcast.1.rank_ref, s32[1,8]{1,0:T(1,128)} %ids_hbm.1, s32[64,4096]{1,0:T(8,128)} %bitcast.25, s32[1,4096]{1,0:T(1,128)} %bitcast.26, f32[8,128,128]{2,1,0:T(8,128)} %bitcast.15), custom_call_target="tpu_custom_call" | custom-call | flops 42949672960 | bytes 8388608 | tf_op jit(solution)/shard_map/count_bags/pallas_call | solution.py:102
  24.4 0.0 collective-permute-done
  24.4 0.0 collective-permute-done.1
  24.4 0.0 collective-permute-done.2
  24.4 0.0 copy-done.4
  24.5 0.1 pad_add_fusion.held_ref
  24.5 0.0 collective-permute-done.5.refs_0_.part1
  24.5 2.0 %pool.2.refs_1_ = f32[1024,128]{1,0:T(8,128)S(1)} custom-call(s32[32]{0:T(128)S(1)} %pad_add_fusion.held_ref, bf16[32,1024,128]{2,1,0:T(8,128)(2,1)S(1)} %get-tuple-element.4.counts_ref, f32[8,128,128]{2,1,0:T(8,128)S(1)} %collective-permute-done.5.refs_0_.part1, f32[8,128,128]{2,1,0:T(8,128)S(1)} %collective-permute-done.3.refs_1_.part2, ...), custom_call_target="tpu_custom_call" | custom-call | flops 1073741824 | bytes 4194304 | tf_op jit(solution)/shard_map/pool/pallas_call | solution.py:142
  26.5 0.0 copy-start.3
  26.5 0.0 copy-start
  26.5 0.0 copy-start.2
  26.5 0.0 copy-start.1
  26.5 0.0 collective-permute-done.4.refs_0_.part3
  26.6 2.1 %pool.3 = f32[1024,128]{1,0:T(8,128)} custom-call(s32[32]{0:T(128)S(1)} %pad_add_fusion.held_ref, bf16[32,1024,128]{2,1,0:T(8,128)(2,1)S(1)} %get-tuple-element.4.counts_ref, f32[8,128,128]{2,1,0:T(8,128)S(1)} %collective-permute-done.4.refs_0_.part3, f32[1024,128]{1,0:T(8,128)S(1)} %pool.2.refs_1_), custom_call_target="tpu_custom_call" | custom-call | flops 536870912 | bytes 4194304 | tf_op jit(solution)/shard_map/pool/pallas_call | solution.py:142
  28.7 14.6 %all-to-all-start = ((f32[64,16,128]{2,1,0:T(8,128)}), f32[64,16,128]{2,1,0:T(8,128)S(1)}, u32[]{:S(2)}, u32[]{:S(2)}) async-start(f32[64,16,128]{2,1,0:T(8,128)} %bitcast.18), calls=%async_computation | async-start | bytes 1048576 | tf_op jit(solution)/shard_map/all_to_all | solution.py:320
  43.3 0.0 copy-done.3
  43.3 0.0 copy-done
  43.3 0.0 copy-done.2
  43.3 1.4 %move_blocks.1 = f32[8,128,128]{2,1,0:T(8,128)} custom-call(s32[32]{0:T(128)S(1)} %pad_add_fusion.held_ref, s32[8]{0:T(128)S(1)} %bitcast.17, f32[8,128,128]{2,1,0:T(8,128)S(1)} %bitcast.16, f32[8,128,128]{2,1,0:T(8,128)S(1)} %collective-permute-done.5.refs_0_.part1, f32[8,128,128]{2,1,0:T(8,128)S(1)} %collective-permute-done.3.refs_1_.part2, ...), custom_call_target="tpu_custom_call" | custom-call | tf_op jit(solution)/shard_map/move_blocks/pallas_call | solution.py:180
  44.7 17.6 %all-to-all-done = f32[64,16,128]{2,1,0:T(8,128)S(1)} async-done(((f32[64,16,128]{2,1,0:T(8,128)}), f32[64,16,128]{2,1,0:T(8,128)S(1)}, u32[]{:S(2)}, u32[]{:S(2)}) %all-to-all-start) | async-done | bytes 524320 | tf_op jit(solution)/shard_map/all_to_all | solution.py:320
  62.3 0.0 copy-done.1
  62.3 4.4 %top_of_model.1 = f32[1,16]{1,0:T(1,128)} custom-call(f32[1024,128]{1,0:T(8,128)S(1)} %bitcast.12, bf16[16,128]{1,0:T(8,128)(2,1)S(1)} %copy-done.1, bf16[2208,1024]{1,0:T(8,128)(2,1)} %first_hbm.1, bf16[1024,1024]{1,0:T(8,128)(2,1)} %second_hbm.1, bf16[1,1024]{1,0:T(2,128)(2,1)S(1)} %reshape.21.out_ref), custom_call_target="tpu_custom_call" | custom-call | tf_op jit(solution)/shard_map/top_of_model/pallas_call | solution.py:269
  (1 shorter events, 0.0 us)
Async XLA Ops:
  0.6 14.0 %collective-permute-start.3 = (f32[8,128,128]{2,1,0:T(8,128)}, f32[8,128,128]{2,1,0:T(8,128)S(1)}, u32[]{:S(2)}, u32[]{:S(2)}) collective-permute-start(f32[8,128,128]{2,1,0:T(8,128)} %bitcast.13), channel_id=1, source_target_pairs={{0,128},{64,192},{128,0},{192,64},{1,129},{65,193},{129,1},{193,65... | collective-permute-start | bytes 1572872 | tf_op jit(solution)/shard_map/ppermute | solution.py:298
  2.2 22.2 %collective-permute-start = (s32[8]{0:T(128)}, s32[8]{0:T(128)S(1)}, u32[]{:S(2)}, u32[]{:S(2)}) collective-permute-start(s32[8]{0:T(128)} %bitcast.21), channel_id=1, source_target_pairs={{0,64},{64,0},{128,192},{192,128},{1,65},{65,1},{129,193},{193,129... | collective-permute-start | bytes 104 | tf_op jit(solution)/shard_map/ppermute | solution.py:302
  2.2 22.2 %collective-permute-start.1 = (s32[8]{0:T(128)}, s32[8]{0:T(128)S(1)}, u32[]{:S(2)}, u32[]{:S(2)}) collective-permute-start(s32[8]{0:T(128)} %bitcast.22), channel_id=1, source_target_pairs={{0,128},{64,192},{128,0},{192,64},{1,129},{65,193},{129,1},{193,65... | collective-permute-start | bytes 104 | tf_op jit(solution)/shard_map/ppermute | solution.py:302
  2.7 21.7 %collective-permute-start.2 = (s32[8]{0:T(128)}, s32[8]{0:T(128)S(1)}, u32[]{:S(2)}, u32[]{:S(2)}) collective-permute-start(s32[8]{0:T(128)} %bitcast.23), channel_id=1, source_target_pairs={{0,192},{64,128},{128,64},{192,0},{1,193},{65,129},{129,65},{193,1... | collective-permute-start | bytes 104 | tf_op jit(solution)/shard_map/ppermute | solution.py:302
  4.1 20.5 %collective-permute-start.5 = (f32[8,128,128]{2,1,0:T(8,128)}, f32[8,128,128]{2,1,0:T(8,128)S(1)}, u32[]{:S(2)}, u32[]{:S(2)}) collective-permute-start(f32[8,128,128]{2,1,0:T(8,128)} %bitcast.14), channel_id=1, source_target_pairs={{0,64},{64,0},{128,192},{192,128},{1,65},{65,1},{129,193},{193,129... | collective-permute-start | bytes 1572872 | tf_op jit(solution)/shard_map/ppermute | solution.py:299
  14.6 11.9 %collective-permute-start.4 = (f32[8,128,128]{2,1,0:T(8,128)S(1)}, f32[8,128,128]{2,1,0:T(8,128)S(1)}, u32[]{:S(2)}, u32[]{:S(2)}) collective-permute-start(f32[8,128,128]{2,1,0:T(8,128)S(1)} %collective-permute-done.3.refs_1_.part2), channel_id=1, source_target_pairs={{0,64},{64,0},{128,192},{192,128},{1,65},{65,1},{129,193},{193,129... | collective-permute-start | bytes 1572872 | tf_op jit(solution)/shard_map/ppermute | solution.py:314
  14.6 9.8 %copy-start.4 = (s32[1,8]{1,0:T(1,128)S(1)}, s32[1,8]{1,0:T(1,128)}, u32[]{:S(2)}) copy-start(s32[1,8]{1,0:T(1,128)} %ids_hbm.1) | copy-start | bytes 100
  26.5 16.8 %copy-start.3 = (bf16[1024]{0:T(1024)(128)(2,1)S(1)}, bf16[1024]{0:T(1024)(128)(2,1)}, u32[]{:S(2)}) copy-start(bf16[1024]{0:T(1024)(128)(2,1)} %param.17) | copy-start | bytes 6148
  26.5 16.8 %copy-start = (f32[1,1024,128]{2,1,0:T(8,128)S(1)}, f32[1,1024,128]{2,1,0:T(8,128)}, u32[]{:S(2)}) copy-start(f32[1,1024,128]{2,1,0:T(8,128)} %param.9) | copy-start | bytes 1572868
  26.5 16.8 %copy-start.2 = (s32[1,8]{1,0:T(1,128)S(1)}, s32[1,8]{1,0:T(1,128)}, u32[]{:S(2)}) copy-start(s32[1,8]{1,0:T(1,128)} %param.11) | copy-start | bytes 100
  26.5 35.7 %copy-start.1 = (bf16[16,128]{1,0:T(8,128)(2,1)S(1)}, bf16[16,128]{1,0:T(8,128)(2,1)}, u32[]{:S(2)}) copy-start(bf16[16,128]{1,0:T(8,128)(2,1)} %dense_ref.1) | copy-start | bytes 12292
  28.7 33.6 %all-to-all-start = ((f32[64,16,128]{2,1,0:T(8,128)}), f32[64,16,128]{2,1,0:T(8,128)S(1)}, u32[]{:S(2)}, u32[]{:S(2)}) async-start(f32[64,16,128]{2,1,0:T(8,128)} %bitcast.18), calls=%async_computation | async-start | bytes 1048576 | tf_op jit(solution)/shard_map/all_to_all | solution.py:320

commit v3 on v2

--- a/solution.py
+++ b/solution.py
@@ -28,7 +28,7 @@
     return pltpu.with_memory_space_constraint(x, pltpu.HBM)
 
 
-def pooled_part(ids, counts_ref, parts, split_rows):
+def pooled_part(ids, counts_ref, parts, split_rows, chunk=None, take=None):
     slots, _, width = parts[0].shape
     for k, part in enumerate(parts):
         for s in range(slots):
@@ -36,9 +36,15 @@
             top, rest = halves(part[s])
             split_rows[at : at + BLK, :width] = top
             split_rows[at : at + BLK, width:] = rest
-    left = jnp.concatenate([counts_ref[b] for b in ids], axis=1)
-    found = jnp.dot(left, split_rows[...], preferred_element_type=F32)
-    return found[:, :width] + found[:, width:]
+    share = counts_ref.shape[1]
+    for m in range(0, share, chunk or share):
+        ends = slice(m, m + (chunk or share))
+        left = jnp.concatenate([counts_ref[b, ends] for b in ids], axis=1)
+        found = jnp.dot(left, split_rows[...], preferred_element_type=F32)
+        found = found[:, :width] + found[:, width:]
+        if take is None:
+            return found
+        take(m, ends, found)
 
 
 def count_kernel(
@@ -124,14 +130,30 @@
     )(rank, in_hbm(ids), in_hbm(index), in_hbm(length), in_hbm(own))
 
 
-def pool_kernel(first_slot, has_prior, held_ref, counts_ref, *refs):
+def pool_kernel(first_slot, has_prior, keep, held_ref, counts_ref, *refs):
     refs = list(refs)
+    sems, sums = (None, None) if keep else (refs.pop(), refs.pop())
     split_rows = refs.pop()
     pooled_ref = refs.pop()
     prior_ref = refs.pop() if has_prior else None
     ids = [held_ref[first_slot + q] for q in range(len(refs) * refs[0].shape[0])]
-    found = pooled_part(ids, counts_ref, refs, split_rows)
-    pooled_ref[...] = found + prior_ref[...] if has_prior else found
+    if keep:
+        found = pooled_part(ids, counts_ref, refs, split_rows)
+        pooled_ref[...] = found + prior_ref[...] if has_prior else found
+        return
+    chunk = pooled_ref.shape[0] // 2
+    sent = []
+
+    def send(m, ends, found):
+        sums[ends] = found + prior_ref[ends] if has_prior else found
+        rows = pl.ds(m, chunk)
+        out = pltpu.make_async_copy(sums.at[rows], pooled_ref.at[rows], sems.at[m // chunk])
+        out.start()
+        sent.append(out)
+
+    pooled_part(ids, counts_ref, refs, split_rows, chunk, send)
+    for out in sent:
+        out.wait()
 
 
 def pool(held, first_slot, counts, parts, prior, keep):
@@ -140,11 +162,12 @@
     vmem = pl.BlockSpec(memory_space=pltpu.VMEM)
     arrays = [counts, *parts] + ([] if prior is None else [prior])
     return pl.pallas_call(
-        functools.partial(pool_kernel, first_slot, prior is not None),
+        functools.partial(pool_kernel, first_slot, prior is not None, keep),
         in_specs=[pl.BlockSpec(memory_space=pltpu.SMEM)] + [vmem] * len(arrays),
-        out_specs=vmem,
+        out_specs=vmem if keep else pl.BlockSpec(memory_space=pltpu.HBM),
         out_shape=pltpu.VMEM((share, width), F32) if keep else pltpu.HBM((share, width), F32),
-        scratch_shapes=[pltpu.VMEM((len(parts) * slots * BLK, 2 * width), BF16)],
+        scratch_shapes=[pltpu.VMEM((len(parts) * slots * BLK, 2 * width), BF16)]
+        + ([] if keep else [pltpu.VMEM((share, width), F32), pltpu.SemaphoreType.DMA((2,))]),
         cost_estimate=pl.CostEstimate(
             flops=2 * share * len(parts) * slots * BLK * 2 * width,
             bytes_accessed=4 << 20,

time: 66.9 us -> 67 us (level)
  no operation moved by 1% of the time
where the time goes in v3:
time: 67 us; the launch traced here: 66.7 us
  waiting for transfers between devices  27.9 us (42%)
  Pallas kernels  19.6 us (29%)
  starting transfers between devices  18.3 us (27%)
  between operations  0.78 us (1%)
    all_to_all x1, waiting for transfers between devices, shards(): lax.all_to_all(pooled, 'col', split_axis=0, concat_axis=0, tiled=True)  17.6 us
    all_to_all x1, starting transfers between devices, shards(): lax.all_to_all(pooled, 'col', split_axis=0, concat_axis=0, tiled=True)  14.6 us
    ppermute x1, waiting for transfers between devices, shards(): across = lax.ppermute(own, 'row', other_chip)  10.2 us
    pallas_call x1, Pallas kernels, count_bags(): pl.pallas_call(count_kernel, in_specs=[pl.BlockSpec(memory_space=pltpu.SM...  9.8 us
    pallas_call x1, Pallas kernels, top_of_model(): pl.pallas_call(top_kernel, in_specs=[vmem, vmem, hbm, hbm, vmem], out_spe...  4.36 us
    pallas_call x2, Pallas kernels, pool(): pl.pallas_call(functools.partial(pool_kernel, first_slot, prior is not No...  4.09 us
    ppermute x3, starting transfers between devices, shards(): named.append(lax.ppermute(ids, 'row', pairs))  1.86 us
    ppermute x1, starting transfers between devices, shards(): across = lax.ppermute(own, 'row', other_chip)  1.58 us
  transfers between devices with their start and end apart: 7, of which 2 were waited for; matrix products, arithmetic and copies ran while one was open for 0% of the time, Pallas kernels for 20%

profile of v3, /device:TPU:8, one launch (start us, length us, event | category | flops | bytes accessed | tf_op | source)
XLA Modules:
  0.0 66.7 jit_solution(6920025747805321378)
XLA Ops:
  0.6 1.6 %collective-permute-start.3 = (f32[8,128,128]{2,1,0:T(8,128)}, f32[8,128,128]{2,1,0:T(8,128)S(1)}, u32[]{:S(2)}, u32[]{:S(2)}) collective-permute-start(f32[8,128,128]{2,1,0:T(8,128)} %bitcast.13), channel_id=1, source_target_pairs={{0,128},{64,192},{128,0},{192,64},{1,129},{65,193},{129,1},{193,65... | collective-permute-start | bytes 1572872 | tf_op jit(solution)/shard_map/ppermute | solution.py:321
  2.2 0.0 collective-permute-start
  2.2 0.5 collective-permute-start.1
  2.7 1.3 %collective-permute-start.2 = (s32[8]{0:T(128)}, s32[8]{0:T(128)S(1)}, u32[]{:S(2)}, u32[]{:S(2)}) collective-permute-start(s32[8]{0:T(128)} %bitcast.23), channel_id=1, source_target_pairs={{0,192},{64,128},{128,64},{192,0},{1,193},{65,129},{129,65},{193,1... | collective-permute-start | bytes 104 | tf_op jit(solution)/shard_map/ppermute | solution.py:325
  4.1 0.3 collective-permute-start.5
  4.4 10.2 %collective-permute-done.3.refs_1_.part2 = f32[8,128,128]{2,1,0:T(8,128)S(1)} collective-permute-done((f32[8,128,128]{2,1,0:T(8,128)}, f32[8,128,128]{2,1,0:T(8,128)S(1)}, u32[]{:S(2)}, u32[]{:S(2)}) %collective-permute-start.3) | collective-permute-done | bytes 524320 | tf_op jit(solution)/shard_map/ppermute | solution.py:321
  14.6 0.0 collective-permute-start.4
  14.6 0.0 copy-start.4
  14.6 9.8 %count_bags.1 = (bf16[32,1024,128]{2,1,0:T(8,128)(2,1)S(1)}, f32[1024,128]{1,0:T(8,128)S(1)}) custom-call(s32[1]{0:T(128)} %bitcast.1.rank_ref, s32[1,8]{1,0:T(1,128)} %ids_hbm.1, s32[64,4096]{1,0:T(8,128)} %bitcast.25, s32[1,4096]{1,0:T(1,128)} %bitcast.26, f32[8,128,128]{2,1,0:T(8,128)} %bitcast.15), custom_call_target="tpu_custom_call" | custom-call | flops 42949672960 | bytes 8388608 | tf_op jit(solution)/shard_map/count_bags/pallas_call | solution.py:108
  24.4 0.0 collective-permute-done
  24.4 0.0 collective-permute-done.1
  24.4 0.0 collective-permute-done.2
  24.4 0.0 copy-done.4
  24.5 0.1 pad_add_fusion.held_ref
  24.5 0.0 collective-permute-done.5.refs_0_.part1
  24.5 2.0 %pool.2.refs_1_ = f32[1024,128]{1,0:T(8,128)S(1)} custom-call(s32[32]{0:T(128)S(1)} %pad_add_fusion.held_ref, bf16[32,1024,128]{2,1,0:T(8,128)(2,1)S(1)} %get-tuple-element.4.counts_ref, f32[8,128,128]{2,1,0:T(8,128)S(1)} %collective-permute-done.5.refs_0_.part1, f32[8,128,128]{2,1,0:T(8,128)S(1)} %collective-permute-done.3.refs_1_.part2, ...), custom_call_target="tpu_custom_call" | custom-call | flops 1073741824 | bytes 4194304 | tf_op jit(solution)/shard_map/pool/pallas_call | solution.py:164
  26.5 0.0 copy-start.3
  26.5 0.0 copy-start
  26.5 0.0 copy-start.2
  26.5 0.0 copy-start.1
  26.5 0.0 collective-permute-done.4.refs_0_.part3
  26.6 2.1 %pool.3 = f32[1024,128]{1,0:T(8,128)} custom-call(s32[32]{0:T(128)S(1)} %pad_add_fusion.held_ref, bf16[32,1024,128]{2,1,0:T(8,128)(2,1)S(1)} %get-tuple-element.4.counts_ref, f32[8,128,128]{2,1,0:T(8,128)S(1)} %collective-permute-done.4.refs_0_.part3, f32[1024,128]{1,0:T(8,128)S(1)} %pool.2.refs_1_), custom_call_target="tpu_custom_call" | custom-call | flops 536870912 | bytes 4194304 | tf_op jit(solution)/shard_map/pool/pallas_call | solution.py:164
  28.7 14.6 %all-to-all-start = ((f32[64,16,128]{2,1,0:T(8,128)}), f32[64,16,128]{2,1,0:T(8,128)S(1)}, u32[]{:S(2)}, u32[]{:S(2)}) async-start(f32[64,16,128]{2,1,0:T(8,128)} %bitcast.18), calls=%async_computation | async-start | bytes 1048576 | tf_op jit(solution)/shard_map/all_to_all | solution.py:343
  43.3 0.0 copy-done.3
  43.3 0.0 copy-done
  43.3 0.0 copy-done.2
  43.3 1.4 %move_blocks.1 = f32[8,128,128]{2,1,0:T(8,128)} custom-call(s32[32]{0:T(128)S(1)} %pad_add_fusion.held_ref, s32[8]{0:T(128)S(1)} %bitcast.17, f32[8,128,128]{2,1,0:T(8,128)S(1)} %bitcast.16, f32[8,128,128]{2,1,0:T(8,128)S(1)} %collective-permute-done.5.refs_0_.part1, f32[8,128,128]{2,1,0:T(8,128)S(1)} %collective-permute-done.3.refs_1_.part2, ...), custom_call_target="tpu_custom_call" | custom-call | tf_op jit(solution)/shard_map/move_blocks/pallas_call | solution.py:203
  44.7 17.6 %all-to-all-done = f32[64,16,128]{2,1,0:T(8,128)S(1)} async-done(((f32[64,16,128]{2,1,0:T(8,128)}), f32[64,16,128]{2,1,0:T(8,128)S(1)}, u32[]{:S(2)}, u32[]{:S(2)}) %all-to-all-start) | async-done | bytes 524320 | tf_op jit(solution)/shard_map/all_to_all | solution.py:343
  62.3 0.0 copy-done.1
  62.3 4.4 %top_of_model.1 = f32[1,16]{1,0:T(1,128)} custom-call(f32[1024,128]{1,0:T(8,128)S(1)} %bitcast.12, bf16[16,128]{1,0:T(8,128)(2,1)S(1)} %copy-done.1, bf16[2208,1024]{1,0:T(8,128)(2,1)} %first_hbm.1, bf16[1024,1024]{1,0:T(8,128)(2,1)} %second_hbm.1, bf16[1,1024]{1,0:T(2,128)(2,1)S(1)} %reshape.21.out_ref), custom_call_target="tpu_custom_call" | custom-call | tf_op jit(solution)/shard_map/top_of_model/pallas_call | solution.py:292
  (1 shorter events, 0.0 us)
Async XLA Ops:
  0.6 14.0 %collective-permute-start.3 = (f32[8,128,128]{2,1,0:T(8,128)}, f32[8,128,128]{2,1,0:T(8,128)S(1)}, u32[]{:S(2)}, u32[]{:S(2)}) collective-permute-start(f32[8,128,128]{2,1,0:T(8,128)} %bitcast.13), channel_id=1, source_target_pairs={{0,128},{64,192},{128,0},{192,64},{1,129},{65,193},{129,1},{193,65... | collective-permute-start | bytes 1572872 | tf_op jit(solution)/shard_map/ppermute | solution.py:321
  2.2 22.2 %collective-permute-start = (s32[8]{0:T(128)}, s32[8]{0:T(128)S(1)}, u32[]{:S(2)}, u32[]{:S(2)}) collective-permute-start(s32[8]{0:T(128)} %bitcast.21), channel_id=1, source_target_pairs={{0,64},{64,0},{128,192},{192,128},{1,65},{65,1},{129,193},{193,129... | collective-permute-start | bytes 104 | tf_op jit(solution)/shard_map/ppermute | solution.py:325
  2.2 22.2 %collective-permute-start.1 = (s32[8]{0:T(128)}, s32[8]{0:T(128)S(1)}, u32[]{:S(2)}, u32[]{:S(2)}) collective-permute-start(s32[8]{0:T(128)} %bitcast.22), channel_id=1, source_target_pairs={{0,128},{64,192},{128,0},{192,64},{1,129},{65,193},{129,1},{193,65... | collective-permute-start | bytes 104 | tf_op jit(solution)/shard_map/ppermute | solution.py:325
  2.7 21.7 %collective-permute-start.2 = (s32[8]{0:T(128)}, s32[8]{0:T(128)S(1)}, u32[]{:S(2)}, u32[]{:S(2)}) collective-permute-start(s32[8]{0:T(128)} %bitcast.23), channel_id=1, source_target_pairs={{0,192},{64,128},{128,64},{192,0},{1,193},{65,129},{129,65},{193,1... | collective-permute-start | bytes 104 | tf_op jit(solution)/shard_map/ppermute | solution.py:325
  4.1 20.5 %collective-permute-start.5 = (f32[8,128,128]{2,1,0:T(8,128)}, f32[8,128,128]{2,1,0:T(8,128)S(1)}, u32[]{:S(2)}, u32[]{:S(2)}) collective-permute-start(f32[8,128,128]{2,1,0:T(8,128)} %bitcast.14), channel_id=1, source_target_pairs={{0,64},{64,0},{128,192},{192,128},{1,65},{65,1},{129,193},{193,129... | collective-permute-start | bytes 1572872 | tf_op jit(solution)/shard_map/ppermute | solution.py:322
  14.6 11.9 %collective-permute-start.4 = (f32[8,128,128]{2,1,0:T(8,128)S(1)}, f32[8,128,128]{2,1,0:T(8,128)S(1)}, u32[]{:S(2)}, u32[]{:S(2)}) collective-permute-start(f32[8,128,128]{2,1,0:T(8,128)S(1)} %collective-permute-done.3.refs_1_.part2), channel_id=1, source_target_pairs={{0,64},{64,0},{128,192},{192,128},{1,65},{65,1},{129,193},{193,129... | collective-permute-start | bytes 1572872 | tf_op jit(solution)/shard_map/ppermute | solution.py:337
  14.6 9.8 %copy-start.4 = (s32[1,8]{1,0:T(1,128)S(1)}, s32[1,8]{1,0:T(1,128)}, u32[]{:S(2)}) copy-start(s32[1,8]{1,0:T(1,128)} %ids_hbm.1) | copy-start | bytes 100
  26.5 16.8 %copy-start.3 = (bf16[1024]{0:T(1024)(128)(2,1)S(1)}, bf16[1024]{0:T(1024)(128)(2,1)}, u32[]{:S(2)}) copy-start(bf16[1024]{0:T(1024)(128)(2,1)} %param.17) | copy-start | bytes 6148
  26.5 16.8 %copy-start = (f32[1,1024,128]{2,1,0:T(8,128)S(1)}, f32[1,1024,128]{2,1,0:T(8,128)}, u32[]{:S(2)}) copy-start(f32[1,1024,128]{2,1,0:T(8,128)} %param.9) | copy-start | bytes 1572868
  26.5 16.8 %copy-start.2 = (s32[1,8]{1,0:T(1,128)S(1)}, s32[1,8]{1,0:T(1,128)}, u32[]{:S(2)}) copy-start(s32[1,8]{1,0:T(1,128)} %param.11) | copy-start | bytes 100
  26.5 35.8 %copy-start.1 = (bf16[16,128]{1,0:T(8,128)(2,1)S(1)}, bf16[16,128]{1,0:T(8,128)(2,1)}, u32[]{:S(2)}) copy-start(bf16[16,128]{1,0:T(8,128)(2,1)} %dense_ref.1) | copy-start | bytes 12292
  28.7 33.6 %all-to-all-start = ((f32[64,16,128]{2,1,0:T(8,128)}), f32[64,16,128]{2,1,0:T(8,128)S(1)}, u32[]{:S(2)}, u32[]{:S(2)}) async-start(f32[64,16,128]{2,1,0:T(8,128)} %bitcast.18), calls=%async_computation | async-start | bytes 1048576 | tf_op jit(solution)/shard_map/all_to_all | solution.py:343
